TPU v7x, 256 devices: a whole 4x4x8 slice. The times are simulated.
256 devices in a mesh: wide: 16 (over z_hi, x), narrow: 4 (over y), depth: 4 (over z_lo, core).
Axes of the slice: x: 4, y: 4, z: 8 (z_hi: 4, z_lo: 2; z = z_hi * 2 + z_lo), core: 2. Of those that a mesh axis runs over, the one named last changes fastest.
Arguments:
- patch_store: bfloat16 [64, 1024, 4096], P('wide', 'depth'), may hold values from -6 to 6
- w_key: bfloat16 [4096, 1024], P(None, 'narrow'), may hold values from -0.09375 to 0.09375
- w_value: bfloat16 [4096, 1024], P(None, 'narrow'), may hold values from -0.09375 to 0.09375
- key_gain: float32 [128], replicated, may hold values from 0.1 to 1.9
- query_gain: float32 [128], replicated, may hold values from 0.1 to 1.9
- queries: bfloat16 [256, 4096], P('wide', 'narrow'), may hold values from -6 to 6
- owner_table: int32 [64], replicated, may hold values from 0 to 63, each once
- reader_table: int32 [16, 2], replicated, may hold values from 0 to 63
- request_image: int32 [256], P('wide'), may hold values from 0 to 1
- image_tiles: int32 [64], replicated, may hold values from 1 to 4
Outputs:
- context: bfloat16 [256, 4096], P(('wide', 'depth'), 'narrow')
Inputs may be any that keep to these rules, and one draw needn't show every extreme that they name: owner_table is a permutation of the slots. `reader_table`: entries are image ids; a group's list may repeat an image.
All inputs are finite; a program needn't handle non-finite values.
Results may differ from a plain program's by a relative error of at most 0.012.
Values may be sent and summed in bfloat16 or wider, within the bound.
A program may use at most 64 MiB of HBM per device.

v0:
```python
import functools
import math

import jax
import jax.numpy as jnp
from jax import lax
from jax.experimental import pallas as pl
from jax.experimental.pallas import tpu as pltpu
from jax.sharding import PartitionSpec as P

HD = 128
TILE_P = 256
EPSILON = 1e-05
CHUNKS = 4
MEET = 0
MESH = pl.DeviceIdType.MESH


def kernel(
    n_wide,
    n_depth,
    store,
    w_key,
    w_value,
    key_gain,
    query_gain,
    queries,
    owner_hbm,
    reader_hbm,
    request_hbm,
    tiles_hbm,
    out,
    owner_table,
    reader_table,
    request_image,
    image_tiles,
    xbuf,
    wbuf,
    qraw,
    gains,
    qf,
    qs,
    qx,
    row_slot,
    row_limit,
    raw,
    keys,
    values,
    msg,
    got,
    res,
    w_sem,
    x_sem,
    q_sem,
    q_send,
    q_recv,
    m_send,
    m_recv,
):
    images, rows, width = xbuf.shape
    kv_local = wbuf.shape[0]
    batch = qraw.shape[0]
    group = qraw.shape[1] // (kv_local * HD)
    share = batch // n_depth
    block = share * group
    group_rows = n_depth * block
    peers = n_wide * n_depth
    total_rows = peers * block
    chunk = width // CHUNKS
    wide, depth = lax.axis_index("wide"), lax.axis_index("depth")
    me = wide * n_depth + depth
    part_lanes = HD // kv_local

    barrier = pltpu.get_barrier_semaphore()

    def peer(offset):
        there = {
            "wide": lax.rem(wide + offset // n_depth, n_wide),
            "depth": lax.rem(depth + offset % n_depth, n_depth),
        }
        return there["wide"] * n_depth + there["depth"], there

    def greet(offset, carry):
        pl.semaphore_signal(barrier, inc=1, device_id=peer(offset)[1], device_id_type=MESH)
        return carry

    lax.fori_loop(1, peers, greet, 0, unroll=peers <= 8)

    def weight_copies(k, c):
        piece = pl.ds(c * chunk, chunk)
        return [
            pltpu.make_async_copy(
                source.at[piece, pl.ds(k * HD, HD)],
                wbuf.at[k, piece, pl.ds(part * HD, HD)],
                w_sem.at[k, c, part],
            )
            for part, source in enumerate((w_key, w_value))
        ]

    def patch_copy(c):
        piece = pl.ds(c * chunk, chunk)
        return pltpu.make_async_copy(store.at[:, :, piece], xbuf.at[:, :, piece], x_sem.at[c])

    small = [
        pltpu.make_async_copy(queries, qraw, q_sem.at[0]),
        pltpu.make_async_copy(query_gain, gains.at[0], q_sem.at[1]),
        pltpu.make_async_copy(key_gain, gains.at[1], q_sem.at[2]),
        pltpu.make_async_copy(owner_hbm, owner_table, q_sem.at[3]),
        pltpu.make_async_copy(reader_hbm, reader_table, q_sem.at[4]),
        pltpu.make_async_copy(request_hbm, request_image, q_sem.at[5]),
        pltpu.make_async_copy(tiles_hbm, image_tiles, q_sem.at[6]),
    ]
    for c in range(CHUNKS):
        for k in range(kv_local):
            for copy in weight_copies(k, c):
                copy.start()
        patch_copy(c).start()
        if c == 0:
            for copy in small:
                copy.start()

    for copy in small:
        copy.wait()
    gain = gains[0] * gains[1] * (1.0 / math.sqrt(HD))
    for h in range(kv_local * group):
        lanes = pl.ds(h * HD, HD)
        head = qraw[:, lanes].astype(jnp.float32)
        mean = jnp.mean(head * head, axis=-1, keepdims=True)
        qf[:, lanes] = head * lax.rsqrt(mean + EPSILON) * gain
    for k in range(kv_local):
        for t in range(n_depth):
            for g in range(group):
                qs[pl.ds(t * block + g * share, share), :] = qf[
                    pl.ds(t * share, share), pl.ds((k * group + g) * HD, HD)
                ]
        qx[wide, k] = qs[...].astype(jnp.bfloat16)
    row = lax.broadcasted_iota(jnp.int32, (group_rows, HD), 0)
    request = row // block * share + row % share
    entry = jnp.zeros((group_rows, HD), jnp.int32)
    for b in range(batch):
        entry = jnp.where(request == b, request_image[b], entry)
    qx[wide, kv_local] = entry.astype(jnp.float32).astype(jnp.bfloat16)

    def query_copy(offset):
        return pltpu.make_async_remote_copy(
            src_ref=qx.at[wide],
            dst_ref=qx.at[wide],
            send_sem=q_send.at[offset],
            recv_sem=q_recv.at[offset],
            device_id={"wide": lax.rem(wide + offset, n_wide)},
            device_id_type=MESH,
        )

    def query_landed(offset):
        source = lax.rem(wide + n_wide - offset, n_wide)
        return pltpu.make_async_remote_copy(
            src_ref=qx.at[source],
            dst_ref=qx.at[source],
            send_sem=q_send.at[offset],
            recv_sem=q_recv.at[offset],
            device_id={"wide": lax.rem(wide + offset, n_wide)},
            device_id_type=MESH,
        )

    def result_copy(offset):
        index, device = peer(offset)
        return pltpu.make_async_remote_copy(
            src_ref=msg.at[index],
            dst_ref=got.at[offset],
            send_sem=m_send.at[offset],
            recv_sem=m_recv.at[offset],
            device_id=device,
            device_id_type=MESH,
        )

    def send_results():
        def step(offset, carry):
            result_copy(offset).start()
            return carry

        lax.fori_loop(1, peers, step, 0, unroll=peers <= 8)

    whole_tiles = TILE_P % rows == 0

    def read_queries():
        for offset in range(1, n_wide):
            query_landed(offset).wait_recv()
        for g in range(n_wide):
            entry = qx[g, kv_local].astype(jnp.float32)
            slots = jnp.full((group_rows, HD), -1, jnp.int32)
            limits = jnp.zeros((group_rows, HD), jnp.int32)
            for r in range(reader_table.shape[1]):
                image = reader_table[g, r]
                slot = owner_table[image]
                limit = image_tiles[image] * TILE_P - depth * rows
                if whole_tiles:
                    slot = jnp.where(limit > 0, slot, -1)
                slots = jnp.where(entry == r, slot, slots)
                limits = jnp.where(entry == r, limit, limits)
            row_slot[pl.ds(g * group_rows, group_rows), :] = slots
            row_limit[pl.ds(g * group_rows, group_rows), :] = limits

    def wider(tile):
        return jnp.concatenate([tile] * (rows // HD), axis=1) if rows > HD else tile

    def prepare(k):
        total = raw[k]
        head = total[:, :HD]
        mean = jnp.mean(head * head, axis=-1, keepdims=True)
        keys[k] = (head * lax.rsqrt(mean + EPSILON)).astype(jnp.bfloat16)
        value = total[:, HD:].astype(jnp.bfloat16)
        values[k] = jnp.concatenate([value, jnp.ones_like(value)], axis=1)

    def attend_groups(k, start, count):
        span = pl.ds(start * group_rows, count * group_rows)
        asked = qx[pl.ds(start, count), k].reshape(count * group_rows, HD)
        wanted, limits = wider(row_slot[span, :]), wider(row_limit[span, :])
        scores = lax.dot_general(
            asked, keys[k], (((1,), (1,)), ((), ())), preferred_element_type=jnp.float32
        )
        weights = []
        for j in range(images):
            keep = wanted == wide * images + j
            if not whole_tiles:
                place = lax.broadcasted_iota(jnp.int32, keep.shape, 1)
                keep = keep & (place < limits)
            part = jnp.exp(scores[:, j * rows : (j + 1) * rows])
            weights.append(jnp.where(keep, part, 0.0).astype(jnp.bfloat16))
        total = jnp.dot(
            jnp.concatenate(weights, axis=1), values[k], preferred_element_type=jnp.float32
        )
        total = total.astype(jnp.bfloat16).reshape(count * n_depth, block, 2 * HD)
        dest = pl.ds(start * n_depth, count * n_depth)
        msg[dest, k] = total[:, :, :HD]
        below = total[:, :, HD:]
        if k:
            lane = lax.broadcasted_iota(jnp.int32, below.shape, 2)
            older = msg[dest, kv_local].astype(jnp.float32)
            below = jnp.where(lane < k * part_lanes, older, below.astype(jnp.float32))
        msg[dest, kv_local] = below.astype(jnp.bfloat16)

    def attend(k):
        if n_wide <= 2:
            attend_groups(k, 0, n_wide)
        else:

            def step(g, carry):
                attend_groups(k, g, 1)
                return carry

            lax.fori_loop(0, n_wide, step, 0)

    def project(k, c):
        piece = pl.ds(c * chunk, chunk)
        part = jnp.dot(
            xbuf[:, :, piece].reshape(images * rows, chunk),
            wbuf[k, piece, :],
            preferred_element_type=jnp.float32,
        )
        raw[k] = part if c == 0 else raw[k] + part

    for c in range(CHUNKS):
        for k in range(kv_local):
            for copy in weight_copies(k, c):
                copy.wait()
        patch_copy(c).wait()
        for k in range(kv_local):
            project(k, c)
            if c == CHUNKS - 1:
                prepare(k)
        if c == min(MEET, CHUNKS - 1):
            pl.semaphore_wait(barrier, peers - 1)
            for offset in range(1, n_wide):
                query_copy(offset).start()
    read_queries()
    for k in range(kv_local):
        attend(k)
    send_results()

    total = msg[me].astype(jnp.float32)

    def collect(offset, total):
        result_copy(offset).wait_recv()
        return total + got[offset].astype(jnp.float32)

    total = lax.fori_loop(1, peers, collect, total, unroll=peers <= 8)
    for k in range(kv_local):
        res[...] = total[k] / total[kv_local, :, k * part_lanes : k * part_lanes + 1]
        for g in range(group):
            out[:, pl.ds((k * group + g) * HD, HD)] = res[pl.ds(g * share, share), :].astype(
                out.dtype
            )

    for offset in range(1, n_wide):
        query_copy(offset).wait_send()

    def drain(offset, carry):
        result_copy(offset).wait_send()
        return carry

    lax.fori_loop(1, peers, drain, 0, unroll=peers <= 8)


def local(
    n_wide,
    n_depth,
    patch_store,
    w_key,
    w_value,
    key_gain,
    query_gain,
    queries,
    owner_table,
    reader_table,
    request_image,
    image_tiles,
):
    images, rows, width = patch_store.shape
    kv_local = w_key.shape[1] // HD
    batch, q_cols = queries.shape
    group = q_cols // (kv_local * HD)
    share = batch // n_depth
    block = share * group
    group_rows = n_depth * block
    peers = n_wide * n_depth
    total_rows = peers * block
    anywhere = pl.BlockSpec(memory_space=pl.ANY)
    dma = pltpu.SemaphoreType.DMA
    return pl.pallas_call(
        functools.partial(kernel, n_wide, n_depth),
        out_shape=pltpu.VMEM((share, q_cols), jnp.bfloat16),
        in_specs=[anywhere] * 10,
        out_specs=pl.BlockSpec(memory_space=pltpu.VMEM),
        scratch_shapes=[
            pltpu.SMEM(owner_table.shape, jnp.int32),
            pltpu.SMEM(reader_table.shape, jnp.int32),
            pltpu.SMEM(request_image.shape, jnp.int32),
            pltpu.SMEM(image_tiles.shape, jnp.int32),
            pltpu.VMEM((images, rows, width), jnp.bfloat16),
            pltpu.VMEM((kv_local, width, 2 * HD), jnp.bfloat16),
            pltpu.VMEM((batch, q_cols), jnp.bfloat16),
            pltpu.VMEM((2, 1, HD), jnp.float32),
            pltpu.VMEM((batch, q_cols), jnp.float32),
            pltpu.VMEM((group_rows, HD), jnp.float32),
            pltpu.VMEM((n_wide, kv_local + 1, group_rows, HD), jnp.bfloat16),
            pltpu.VMEM((total_rows, HD), jnp.int32),
            pltpu.VMEM((total_rows, HD), jnp.int32),
            pltpu.VMEM((kv_local, images * rows, 2 * HD), jnp.float32),
            pltpu.VMEM((kv_local, images * rows, HD), jnp.bfloat16),
            pltpu.VMEM((kv_local, images * rows, 2 * HD), jnp.bfloat16),
            pltpu.VMEM((peers, kv_local + 1, block, HD), jnp.bfloat16),
            pltpu.VMEM((peers, kv_local + 1, block, HD), jnp.bfloat16),
            pltpu.VMEM((block, HD), jnp.float32),
            dma((kv_local, CHUNKS, 2)),
            dma((CHUNKS,)),
            dma((7,)),
            dma((n_wide,)),
            dma((n_wide,)),
            dma((peers,)),
            dma((peers,)),
        ],
        compiler_params=pltpu.CompilerParams(
            collective_id=0, has_side_effects=True, vmem_limit_bytes=56 * 1024 * 1024
        ),
    )(
        patch_store,
        w_key,
        w_value,
        key_gain.reshape(1, HD),
        query_gain.reshape(1, HD),
        queries,
        owner_table,
        reader_table,
        request_image,
        image_tiles,
    )


def solution(mesh):
    placed = (
        P("wide", "depth", None),
        P(None, "narrow"),
        P(None, "narrow"),
        P(),
        P(),
        P("wide", "narrow"),
        P(),
        P(),
        P("wide"),
        P(),
    )
    return jax.shard_map(
        functools.partial(local, mesh.shape["wide"], mesh.shape["depth"]),
        mesh=mesh,
        in_specs=placed,
        out_specs=P(("wide", "depth"), "narrow"),
        check_vma=False,
    )
```

profile of v0, /device:TPU:1, one launch (start us, length us, event | category | flops | bytes accessed | tf_op | source)
XLA Modules:
  0.0 65.3 jit_solution(8090644754878557773)
XLA Ops:
  0.0 1.4 %copy.11.reader_hbm = s32[16,2]{1,0:T(8,128)} copy(s32[16,2]{0,1:T(2,128)} %param.17) | data formatting | bytes 256 | tf_op args[7]
  1.4 63.4 %shard_map.100 = bf16[4,1024]{1,0:T(4,128)(2,1)S(1)} custom-call(bf16[4,256,4096]{2,1,0:T(8,128)(2,1)} %store.1, bf16[4096,256]{1,0:T(8,128)(2,1)} %w_key.1, bf16[4096,256]{1,0:T(8,128)(2,1)} %w_value.1, f32[1,128]{1,0:T(1,128)} %bitcast.2, f32[1,128]{1,0:T(1,128)} %bitcast.3, bf16[16,1024]{1,0:T(8,128)(2,1)} %queries.1, s32[64]{0:T(128)} %owner_hbm.1, ...), custom_call_target="tpu_custom_call" | custom-call | tf_op jit(solution)/shard_map/pallas_call | solution.py:329
  64.7 0.6 copy.13
where the time goes:
time: 66.1 us; the launch traced here: 65.3 us
  Pallas kernels  63.4 us (96%)
  local copies, waits for them, and re-layouts  1.95 us (3%)
    pallas_call x1, Pallas kernels, local(): pl.pallas_call(functools.partial(kernel, n_wide, n_depth), out_shape=pltp...  63.4 us
    unnamed x2, local copies, waits for them, and re-layouts  1.95 us

commit v1 on v0

v1 whole, which is shorter than its diff:
```python
import functools
import math

import jax
import jax.numpy as jnp
from jax import lax
from jax.experimental import pallas as pl
from jax.experimental.pallas import tpu as pltpu
from jax.sharding import PartitionSpec as P

HD = 128
EPSILON = 1e-05
CHUNKS = 4
XS = 4
ZS = 8
CORES = 2
GROUP = 4
SHARE = 4
ROWS = 64
OUTSIDE = -30000.0
MESH = pl.DeviceIdType.MESH


def kernel(
    store,
    w_key,
    w_value,
    key_gain,
    query_gain,
    queries,
    owner_hbm,
    reader_hbm,
    request_hbm,
    tiles_hbm,
    out,
    owner_table,
    reader_table,
    request_image,
    image_tiles,
    xbuf,
    wbuf,
    qraw,
    gains,
    qf,
    qs,
    qx,
    ids,
    raw,
    kvout,
    kbuf,
    vbuf,
    kext,
    mnum,
    mden,
    xnum,
    xden,
    znum,
    zden,
    gnum,
    gden,
    res,
    w_sem,
    x_sem,
    small_sem,
    qz_send,
    qz_recv,
    qx_send,
    qx_recv,
    kv_send,
    kv_recv,
    rx_send,
    rx_recv,
    rz_send,
    rz_recv,
):
    images, rows, width = xbuf.shape
    batch = qraw.shape[0]
    chunk = width // CHUNKS
    pairs = ZS // 2
    wide, depth = lax.axis_index("wide"), lax.axis_index("depth")
    zh, x = wide // XS, lax.rem(wide, XS)
    zl, core = depth // CORES, lax.rem(depth, CORES)
    other = 1 - core
    z = zh * 2 + zl

    barrier = pltpu.get_barrier_semaphore()

    def x_mate(o):
        return {"wide": zh * XS + lax.rem(x + o, XS), "depth": depth}

    def z_place(dz, dc):
        there = lax.rem(z + dz, ZS)
        return there // 2, lax.rem(there, 2) * CORES + lax.rem(core + dc, CORES)

    def z_mate(dz, dc):
        pair, part = z_place(dz, dc)
        return {"wide": pair * XS + x, "depth": part}

    z_mates = [(dz, dc) for dz in range(ZS) for dc in range(CORES) if dz or dc]

    for o in range(1, XS):
        pl.semaphore_signal(barrier, inc=1, device_id=x_mate(o), device_id_type=MESH)
    for dz, dc in z_mates:
        pl.semaphore_signal(barrier, inc=1, device_id=z_mate(dz, dc), device_id_type=MESH)

    def head_lanes(which):
        return pl.ds(pl.multiple_of(which * HD, HD), HD)

    def weight_copies(slot, c):
        piece = pl.ds(c * chunk, chunk)
        which = core if slot == 0 else other
        return [
            pltpu.make_async_copy(
                source.at[piece, head_lanes(which)],
                wbuf.at[slot, piece, pl.ds(part * HD, HD)],
                w_sem.at[slot, c, part],
            )
            for part, source in enumerate((w_key, w_value))
        ]

    def patch_copy(c):
        piece = pl.ds(c * chunk, chunk)
        return pltpu.make_async_copy(store.at[:, :, piece], xbuf.at[:, :, piece], x_sem.at[c])

    mine = pl.ds(pl.multiple_of(core * GROUP * HD, HD), GROUP * HD)
    small = [
        pltpu.make_async_copy(queries.at[:, mine], qraw, small_sem.at[0]),
        pltpu.make_async_copy(query_gain, gains.at[0], small_sem.at[1]),
        pltpu.make_async_copy(key_gain, gains.at[1], small_sem.at[2]),
        pltpu.make_async_copy(owner_hbm, owner_table, small_sem.at[3]),
        pltpu.make_async_copy(reader_hbm, reader_table, small_sem.at[4]),
        pltpu.make_async_copy(request_hbm, request_image, small_sem.at[5]),
        pltpu.make_async_copy(tiles_hbm, image_tiles, small_sem.at[6]),
    ]
    for copy in small:
        copy.start()
    for c in range(CHUNKS):
        for copy in weight_copies(1, c):
            copy.start()
        patch_copy(c).start()
    for c in range(CHUNKS):
        for copy in weight_copies(0, c):
            copy.start()
    for copy in small:
        copy.wait()

    gain = gains[0] * gains[1] * (math.log2(math.e) / math.sqrt(HD))
    for h in range(GROUP):
        head = qraw[:, h * HD : (h + 1) * HD].astype(jnp.float32)
        mean = jnp.mean(head * head, axis=-1, keepdims=True)
        qf[h] = head * lax.rsqrt(mean + EPSILON) * gain
    for t in range(batch // SHARE):
        for h in range(GROUP):
            qs[pl.ds(t * 16 + h * SHARE, SHARE), :] = qf[h, pl.ds(t * SHARE, SHARE), :]
    qx[x, zh] = qs[...].astype(jnp.bfloat16)

    lane = lax.broadcasted_iota(jnp.int32, (1, HD), 1)
    request = lax.rem(lane, ROWS) // 16 * SHARE + lax.rem(lane, SHARE)
    first, second = reader_table[wide, 0], reader_table[wide, 1]
    image = jnp.zeros((1, HD), jnp.int32)
    for b in range(batch):
        image = jnp.where(request == b, jnp.where(request_image[b] == 0, first, second), image)
    ids[x, zh] = image.astype(jnp.float32)

    owner = jnp.full((1, HD), -1, jnp.int32)
    tiles = jnp.zeros((1, HD), jnp.int32)
    for m in range(owner_table.shape[0]):
        owner = jnp.where(lane == m, owner_table[m], owner)
        tiles = jnp.where(lane == m, image_tiles[m], tiles)
    for half, part in enumerate((depth, zl * CORES + other)):
        for j in range(images):
            usable = (owner == wide * images + j) & (tiles > part)
            line = jnp.where(usable, 0.0, OUTSIDE)
            kext[half, j] = jnp.broadcast_to(line, (rows, HD)).astype(jnp.bfloat16)

    def query_pieces(column, pair):
        return (qx.at[column, pair], ids.at[column, pair])

    def query_z(n):
        step = jnp.where(zl == 1, 1, pairs - 1)
        pair = lax.rem(zh + (step if n < 2 else 2), pairs)
        there = n if n < 2 else 1 - zl
        device = {"wide": pair * XS + x, "depth": there * CORES + core}
        return [
            pltpu.make_async_remote_copy(
                src_ref=ref,
                dst_ref=ref,
                send_sem=qz_send.at[n, i],
                recv_sem=qz_recv.at[zh, i],
                device_id=device,
                device_id_type=MESH,
            )
            for i, ref in enumerate(query_pieces(x, zh))
        ]

    def query_z_landed(dz):
        pair = lax.rem(zh + dz, pairs)
        return [
            pltpu.make_async_remote_copy(
                src_ref=ref,
                dst_ref=ref,
                send_sem=qz_send.at[0, i],
                recv_sem=qz_recv.at[pair, i],
                device_id=x_mate(1),
                device_id_type=MESH,
            )
            for i, ref in enumerate(query_pieces(x, pair))
        ]

    def query_x(o, dz, back=False):
        pair = lax.rem(zh + dz, pairs)
        column = lax.rem(x + (XS - o if back else 0), XS)
        return [
            pltpu.make_async_remote_copy(
                src_ref=ref,
                dst_ref=ref,
                send_sem=qx_send.at[o, dz, i],
                recv_sem=qx_recv.at[o, dz, i],
                device_id=x_mate(o),
                device_id_type=MESH,
            )
            for i, ref in enumerate(query_pieces(column, pair))
        ]

    def project_other(c):
        piece = pl.ds(c * chunk, chunk)
        part = jnp.dot(
            xbuf[:, :, piece].reshape(images * rows, chunk),
            wbuf[1, piece, :],
            preferred_element_type=jnp.float32,
        )
        raw[...] = part if c == 0 else raw[...] + part

    def normed_keys(head):
        mean = jnp.mean(head * head, axis=-1, keepdims=True)
        return (head * lax.rsqrt(mean + EPSILON)).astype(jnp.bfloat16)

    def kv_copies(j):
        return [
            pltpu.make_async_remote_copy(
                src_ref=kvout.at[part, j],
                dst_ref=into.at[1, j],
                send_sem=kv_send.at[part, j],
                recv_sem=kv_recv.at[part, j],
                device_id={"depth": zl * CORES + other},
                device_id_type=MESH,
            )
            for part, into in enumerate((kbuf, vbuf))
        ]

    for c in range(CHUNKS):
        for copy in weight_copies(1, c):
            copy.wait()
        patch_copy(c).wait()
        project_other(c)
        if c == 0:
            pl.semaphore_wait(barrier, XS - 1 + len(z_mates))
            for n in (2, 1, 0):
                for copy in query_z(n):
                    copy.start()
            for o in (2, 1, 3):
                for copy in query_x(o, 0):
                    copy.start()
    for j in range(images):
        total = raw[j * rows : (j + 1) * rows, :]
        kvout[0, j] = normed_keys(total[:, :HD])
        kvout[1, j] = total[:, HD:].astype(jnp.bfloat16)
        for copy in kv_copies(j):
            copy.start()

    for c in range(CHUNKS):
        for copy in weight_copies(0, c):
            copy.wait()
    for j in range(images):
        total = jnp.dot(xbuf[j], wbuf[0], preferred_element_type=jnp.float32)
        kbuf[0, j] = normed_keys(total[:, :HD])
        vbuf[0, j] = total[:, HD:].astype(jnp.bfloat16)

    for dz in (1, 3, 2):
        for copy in query_z_landed(dz):
            copy.wait_recv()
        for o in (2, 1, 3):
            for copy in query_x(o, dz):
                copy.start()

    for j in range(images):
        for copy in kv_copies(j):
            copy.wait_recv()

    row = lax.broadcasted_iota(jnp.int32, (HD, HD), 0)
    column_of = lax.broadcasted_iota(jnp.int32, (HD, HD), 1)
    diagonal = row == column_of
    lane_value = column_of.astype(jnp.float32)

    def attend(column):
        chosen = []
        for pair in range(pairs):
            spread = jnp.broadcast_to(ids[column, pair], (ROWS, HD))
            image = jnp.sum(
                jnp.where(diagonal[:ROWS], spread, 0.0), axis=1, keepdims=True
            )
            chosen.append(jnp.where(lane_value[:ROWS] == image, 1.0, 0.0).astype(jnp.bfloat16))
        asked = jnp.concatenate(
            [qx[column].reshape(pairs * ROWS, HD), jnp.concatenate(chosen, axis=0)], axis=1
        )
        weights, worth = [], []
        for half in range(CORES):
            for j in range(images):
                scores = lax.dot_general(
                    asked,
                    jnp.concatenate([kbuf[half, j], kext[half, j]], axis=1),
                    (((1,), (1,)), ((), ())),
                    preferred_element_type=jnp.float32,
                )
                weights.append(jnp.exp2(scores).astype(jnp.bfloat16))
                value = vbuf[half, j]
                worth.append(jnp.concatenate([value, jnp.ones_like(value)], axis=1))
        total = jnp.dot(
            jnp.concatenate(weights, axis=1),
            jnp.concatenate(worth, axis=0),
            preferred_element_type=jnp.float32,
        )
        mnum[column] = total[:, :HD].astype(jnp.bfloat16)
        for part in range(2):
            below = total[part * HD : (part + 1) * HD, HD:]
            mden[column, part] = jnp.sum(
                jnp.where(diagonal, below, 0.0), axis=0, keepdims=True
            )

    def result_x(o):
        column = lax.rem(x + o, XS)
        return [
            pltpu.make_async_remote_copy(
                src_ref=source.at[column],
                dst_ref=into.at[o],
                send_sem=rx_send.at[o, i],
                recv_sem=rx_recv.at[o, i],
                device_id=x_mate(o),
                device_id_type=MESH,
            )
            for i, (source, into) in enumerate(((mnum, xnum), (mden, xden)))
        ]

    attend(x)
    for o in (1, 3, 2):
        for dz in (0, 1, 3, 2):
            for copy in query_x(o, dz, back=True):
                copy.wait_recv()
        attend(lax.rem(x + XS - o, XS))
        for copy in result_x(XS - o):
            copy.start()

    number = mnum[x].astype(jnp.float32)
    below = mden[x]
    for o in (3, 1, 2):
        for copy in result_x(o):
            copy.wait_recv()
        number = number + xnum[o].astype(jnp.float32)
        below = below + xden[o]
    znum[...] = number.astype(jnp.bfloat16).reshape(znum.shape)
    zden[...] = below

    def result_z(dz, dc):
        pair, part = z_place(dz, dc)
        return [
            pltpu.make_async_remote_copy(
                src_ref=source,
                dst_ref=into.at[core, dz],
                send_sem=rz_send.at[dz, dc, i],
                recv_sem=rz_recv.at[dz, dc, i],
                device_id=z_mate(dz, dc),
                device_id_type=MESH,
            )
            for i, (source, into) in enumerate(
                ((znum.at[pair, part], gnum), (zden.at[pair // 2], gden))
            )
        ]

    for dz, dc in sorted(z_mates, key=lambda m: -min(m[0], ZS - m[0])):
        for copy in result_z(dz, dc):
            copy.start()
    gnum[core, 0] = znum[zh, depth]
    gden[core, 0] = zden[zh // 2]
    for dz, dc in sorted(z_mates, key=lambda m: min(m[0], ZS - m[0])):
        for copy in result_z(dz, dc):
            copy.wait_recv()

    place = lax.rem(zh, 2) * ROWS + depth * 16
    here = column_of[:16] == row[:16] + place
    for k in range(CORES):
        number = gnum[k, 0].astype(jnp.float32)
        below = gden[k, 0]
        for dz in range(1, ZS):
            number = number + gnum[k, dz].astype(jnp.float32)
            below = below + gden[k, dz]
        spread = jnp.where(here, jnp.broadcast_to(below, (16, HD)), 0.0)
        res[...] = number / jnp.sum(spread, axis=1, keepdims=True)
        for h in range(GROUP):
            out[:, pl.ds((k * GROUP + h) * HD, HD)] = res[pl.ds(h * SHARE, SHARE), :].astype(
                out.dtype
            )

    for n in range(3):
        for copy in query_z(n):
            copy.wait_send()
    for o in range(1, XS):
        for dz in range(pairs):
            for copy in query_x(o, dz):
                copy.wait_send()
        for copy in result_x(o):
            copy.wait_send()
    for j in range(images):
        for copy in kv_copies(j):
            copy.wait_send()
    for dz, dc in z_mates:
        for copy in result_z(dz, dc):
            copy.wait_send()


def local(
    patch_store,
    w_key,
    w_value,
    key_gain,
    query_gain,
    queries,
    owner_table,
    reader_table,
    request_image,
    image_tiles,
):
    images, rows, width = patch_store.shape
    batch, q_cols = queries.shape
    anywhere = pl.BlockSpec(memory_space=pl.ANY)
    dma = pltpu.SemaphoreType.DMA
    bf16, f32 = jnp.bfloat16, jnp.float32
    pairs = ZS // 2
    return pl.pallas_call(
        kernel,
        out_shape=pltpu.VMEM((SHARE, q_cols), bf16),
        in_specs=[anywhere] * 10,
        out_specs=pl.BlockSpec(memory_space=pltpu.VMEM),
        scratch_shapes=[
            pltpu.SMEM(owner_table.shape, jnp.int32),
            pltpu.SMEM(reader_table.shape, jnp.int32),
            pltpu.SMEM(request_image.shape, jnp.int32),
            pltpu.SMEM(image_tiles.shape, jnp.int32),
            pltpu.VMEM((images, rows, width), bf16),
            pltpu.VMEM((2, width, 2 * HD), bf16),
            pltpu.VMEM((batch, GROUP * HD), bf16),
            pltpu.VMEM((2, 1, HD), f32),
            pltpu.VMEM((GROUP, batch, HD), f32),
            pltpu.VMEM((ROWS, HD), f32),
            pltpu.VMEM((XS, pairs, ROWS, HD), bf16),
            pltpu.VMEM((XS, pairs, 1, HD), f32),
            pltpu.VMEM((images * rows, 2 * HD), f32),
            pltpu.VMEM((2, images, rows, HD), bf16),
            pltpu.VMEM((CORES, images, rows, HD), bf16),
            pltpu.VMEM((CORES, images, rows, HD), bf16),
            pltpu.VMEM((CORES, images, rows, HD), bf16),
            pltpu.VMEM((XS, pairs * ROWS, HD), bf16),
            pltpu.VMEM((XS, 2, 1, HD), f32),
            pltpu.VMEM((XS, pairs * ROWS, HD), bf16),
            pltpu.VMEM((XS, 2, 1, HD), f32),
            pltpu.VMEM((pairs, 2 * CORES, 16, HD), bf16),
            pltpu.VMEM((2, 1, HD), f32),
            pltpu.VMEM((CORES, ZS, 16, HD), bf16),
            pltpu.VMEM((CORES, ZS, 1, HD), f32),
            pltpu.VMEM((16, HD), f32),
            dma((2, CHUNKS, 2)),
            dma((CHUNKS,)),
            dma((7,)),
            dma((3, 2)),
            dma((pairs, 2)),
            dma((XS, pairs, 2)),
            dma((XS, pairs, 2)),
            dma((2, images)),
            dma((2, images)),
            dma((XS, 2)),
            dma((XS, 2)),
            dma((ZS, CORES, 2)),
            dma((ZS, CORES, 2)),
        ],
        compiler_params=pltpu.CompilerParams(
            collective_id=0, has_side_effects=True, vmem_limit_bytes=56 * 1024 * 1024
        ),
    )(
        patch_store,
        w_key,
        w_value,
        key_gain.reshape(1, HD),
        query_gain.reshape(1, HD),
        queries,
        owner_table,
        reader_table,
        request_image,
        image_tiles,
    )


def solution(mesh):
    placed = (
        P("wide", "depth", None),
        P(None, "narrow"),
        P(None, "narrow"),
        P(),
        P(),
        P("wide", "narrow"),
        P(),
        P(),
        P("wide"),
        P(),
    )
    return jax.shard_map(
        local,
        mesh=mesh,
        in_specs=placed,
        out_specs=P(("wide", "depth"), "narrow"),
        check_vma=False,
    )
```

time: 66.1 us -> 37.1 us (0.56); the launches traced: 65.3 us -> 37 us
  Pallas kernels: 63.4 us -> 35 us
    pallas_call x1, Pallas kernels: 63.4 us -> 35 us  [local(): pl.pallas_call(kernel, out_shape=pltpu.VMEM((SHARE, q_cols), bf16), in_sp...]
where the time goes in v1:
time: 37.1 us; the launch traced here: 37 us
  Pallas kernels  35 us (94%)
  local copies, waits for them, and re-layouts  1.95 us (5%)
    pallas_call x1, Pallas kernels, local(): pl.pallas_call(kernel, out_shape=pltpu.VMEM((SHARE, q_cols), bf16), in_sp...  35 us
    unnamed x2, local copies, waits for them, and re-layouts  1.95 us

profile of v1, /device:TPU:1, one launch (start us, length us, event | category | flops | bytes accessed | tf_op | source)
XLA Modules:
  0.0 37.0 jit_solution(3558238005648102852)
XLA Ops:
  0.0 1.4 %copy.11.reader_hbm = s32[16,2]{1,0:T(8,128)} copy(s32[16,2]{0,1:T(2,128)} %param.17) | data formatting | bytes 256 | tf_op args[7]
  1.4 35.0 %shard_map.100 = bf16[4,1024]{1,0:T(4,128)(2,1)S(1)} custom-call(bf16[4,256,4096]{2,1,0:T(8,128)(2,1)} %store.1, bf16[4096,256]{1,0:T(8,128)(2,1)} %w_key.1, bf16[4096,256]{1,0:T(8,128)(2,1)} %w_value.1, f32[1,128]{1,0:T(1,128)} %bitcast.2, f32[1,128]{1,0:T(1,128)} %bitcast.3, bf16[16,1024]{1,0:T(8,128)(2,1)} %queries.1, s32[64]{0:T(128)} %owner_hbm.1, ...), custom_call_target="tpu_custom_call" | custom-call | tf_op jit(solution)/shard_map/pallas_call | solution.py:438
  36.4 0.6 %copy.13 = bf16[4,1024]{1,0:T(4,128)(2,1)} copy(bf16[4,1024]{1,0:T(4,128)(2,1)S(1)} %shard_map.100) | data formatting | bytes 16384

commit v2 on v1

v2 whole, which is shorter than its diff:
```python
import functools
import math

import jax
import jax.numpy as jnp
from jax import lax
from jax.experimental import pallas as pl
from jax.experimental.pallas import tpu as pltpu
from jax.sharding import PartitionSpec as P

HD = 128
EPSILON = 1e-05
CHUNKS = 4
XS = 4
ZS = 8
CORES = 2
GROUP = 4
SHARE = 4
ROWS = 64
OUTSIDE = -30000.0
MESH = pl.DeviceIdType.MESH


def kernel(
    store,
    w_key,
    w_value,
    key_gain,
    query_gain,
    queries,
    owner_hbm,
    reader_hbm,
    request_hbm,
    tiles_hbm,
    out,
    owner_table,
    reader_table,
    request_image,
    image_tiles,
    xbuf,
    wbuf,
    qraw,
    gains,
    qf,
    qs,
    qx,
    ids,
    raw,
    kvout,
    kbuf,
    vbuf,
    kext,
    mnum,
    mden,
    xnum,
    xden,
    znum,
    zden,
    gnum,
    gden,
    res,
    w_sem,
    x_sem,
    small_sem,
    qz_send,
    qz_recv,
    qx_send,
    qx_recv,
    kv_send,
    kv_recv,
    rx_send,
    rx_recv,
    rz_send,
    rz_recv,
):
    images, rows, width = xbuf.shape
    batch = qraw.shape[0]
    chunk = width // CHUNKS
    pairs = ZS // 2
    wide, depth = lax.axis_index("wide"), lax.axis_index("depth")
    zh, x = wide // XS, lax.rem(wide, XS)
    zl, core = depth // CORES, lax.rem(depth, CORES)
    other = 1 - core
    z = zh * 2 + zl

    barrier = pltpu.get_barrier_semaphore()

    def x_mate(o):
        return {"wide": zh * XS + lax.rem(x + o, XS), "depth": depth}

    def z_mate(dz, dc):
        there = lax.rem(z + dz, ZS)
        part = lax.rem(there, 2) * CORES + lax.rem(core + dc, CORES)
        return {"wide": there // 2 * XS + x, "depth": part}

    z_mates = [(dz, dc) for dz in range(ZS) for dc in range(CORES) if dz or dc]

    for o in range(1, XS):
        pl.semaphore_signal(barrier, inc=1, device_id=x_mate(o), device_id_type=MESH)
    for dz, dc in z_mates:
        pl.semaphore_signal(barrier, inc=1, device_id=z_mate(dz, dc), device_id_type=MESH)

    def head_lanes(which):
        return pl.ds(pl.multiple_of(which * HD, HD), HD)

    def weight_copies(c):
        piece = pl.ds(c * chunk, chunk)
        return [
            pltpu.make_async_copy(
                source.at[piece, head_lanes(which)],
                wbuf.at[piece, pl.ds((2 * slot + part) * HD, HD)],
                w_sem.at[slot, c, part],
            )
            for slot, which in enumerate((core, other))
            for part, source in enumerate((w_key, w_value))
        ]

    def patch_copy(c):
        if c < CHUNKS:
            place = (pl.ds(0, 2), slice(None), pl.ds(c * chunk, chunk))
        else:
            place = (c - CHUNKS + 2,)
        return pltpu.make_async_copy(store.at[place], xbuf.at[place], x_sem.at[c])

    mine = pl.ds(pl.multiple_of(core * GROUP * HD, HD), GROUP * HD)
    small = [
        pltpu.make_async_copy(queries.at[:, mine], qraw, small_sem.at[0]),
        pltpu.make_async_copy(query_gain, gains.at[0], small_sem.at[1]),
        pltpu.make_async_copy(key_gain, gains.at[1], small_sem.at[2]),
        pltpu.make_async_copy(owner_hbm, owner_table, small_sem.at[3]),
        pltpu.make_async_copy(reader_hbm, reader_table, small_sem.at[4]),
        pltpu.make_async_copy(request_hbm, request_image, small_sem.at[5]),
        pltpu.make_async_copy(tiles_hbm, image_tiles, small_sem.at[6]),
    ]
    for copy in small:
        copy.start()
    for c in range(CHUNKS):
        for copy in weight_copies(c):
            copy.start()
        patch_copy(c).start()
    for j in range(2, images):
        patch_copy(CHUNKS + j - 2).start()
    for copy in small:
        copy.wait()

    gain = gains[0] * gains[1] * (math.log2(math.e) / math.sqrt(HD))
    for h in range(GROUP):
        head = qraw[:, h * HD : (h + 1) * HD].astype(jnp.float32)
        mean = jnp.mean(head * head, axis=-1, keepdims=True)
        qf[h] = head * lax.rsqrt(mean + EPSILON) * gain
    for t in range(batch // SHARE):
        for h in range(GROUP):
            qs[pl.ds(t * 16 + h * SHARE, SHARE), :] = qf[h, pl.ds(t * SHARE, SHARE), :]
    qx[zh, x] = qs[...].astype(jnp.bfloat16)

    lane = lax.broadcasted_iota(jnp.int32, (1, HD), 1)
    request = lax.rem(lane, ROWS) // 16 * SHARE + lax.rem(lane, SHARE)
    first, second = reader_table[0, wide], reader_table[1, wide]
    image = jnp.zeros((1, HD), jnp.int32)
    for b in range(batch):
        image = jnp.where(request == b, jnp.where(request_image[b] == 0, first, second), image)
    ids[zh, x] = image.astype(jnp.float32)

    owner = jnp.full((1, HD), -1, jnp.int32)
    tiles = jnp.zeros((1, HD), jnp.int32)
    for m in range(owner_table.shape[0]):
        owner = jnp.where(lane == m, owner_table[m], owner)
        tiles = jnp.where(lane == m, image_tiles[m], tiles)
    for half, part in enumerate((depth, zl * CORES + other)):
        for j in range(images):
            usable = (owner == wide * images + j) & (tiles > part)
            line = jnp.where(usable, 0.0, OUTSIDE)
            kext[half, j] = jnp.broadcast_to(line, (rows, HD)).astype(jnp.bfloat16)

    def query_pieces(pair, column):
        return (qx.at[pair, column], ids.at[pair, column])

    def query_z(n):
        step = jnp.where(zl == 1, 1, pairs - 1)
        pair = lax.rem(zh + (step if n < 2 else 2), pairs)
        there = n if n < 2 else 1 - zl
        device = {"wide": pair * XS + x, "depth": there * CORES + core}
        return [
            pltpu.make_async_remote_copy(
                src_ref=ref,
                dst_ref=ref,
                send_sem=qz_send.at[n, i],
                recv_sem=qz_recv.at[zh, i],
                device_id=device,
                device_id_type=MESH,
            )
            for i, ref in enumerate(query_pieces(zh, x))
        ]

    def query_z_landed(dz):
        pair = lax.rem(zh + dz, pairs)
        return [
            pltpu.make_async_remote_copy(
                src_ref=ref,
                dst_ref=ref,
                send_sem=qz_send.at[0, i],
                recv_sem=qz_recv.at[pair, i],
                device_id=x_mate(1),
                device_id_type=MESH,
            )
            for i, ref in enumerate(query_pieces(pair, x))
        ]

    def query_x(o, dz, back=False):
        pair = lax.rem(zh + dz, pairs)
        column = lax.rem(x + (XS - o if back else 0), XS)
        return [
            pltpu.make_async_remote_copy(
                src_ref=ref,
                dst_ref=ref,
                send_sem=qx_send.at[o, dz, i],
                recv_sem=qx_recv.at[o, dz, i],
                device_id=x_mate(o),
                device_id_type=MESH,
            )
            for i, ref in enumerate(query_pieces(pair, column))
        ]

    def forward(dz):
        if dz:
            for copy in query_z_landed(dz):
                copy.wait_recv()
        for o in (2, 1, 3):
            for copy in query_x(o, dz):
                copy.start()

    def project_pair(c):
        piece = pl.ds(c * chunk, chunk)
        part = jnp.dot(
            xbuf[:2, :, piece].reshape(2 * rows, chunk),
            wbuf[piece, :],
            preferred_element_type=jnp.float32,
        )
        raw[...] = part if c == 0 else raw[...] + part

    def normed_keys(head):
        mean = jnp.mean(head * head, axis=-1, keepdims=True)
        return (head * lax.rsqrt(mean + EPSILON)).astype(jnp.bfloat16)

    def kv_copies(j):
        return [
            pltpu.make_async_remote_copy(
                src_ref=kvout.at[part, j],
                dst_ref=into.at[1, j],
                send_sem=kv_send.at[part, j],
                recv_sem=kv_recv.at[part, j],
                device_id={"depth": zl * CORES + other},
                device_id_type=MESH,
            )
            for part, into in enumerate((kbuf, vbuf))
        ]

    def keep_kv(j, total):
        kvout[0, j] = normed_keys(total[:, 2 * HD : 3 * HD])
        kvout[1, j] = total[:, 3 * HD :].astype(jnp.bfloat16)
        for copy in kv_copies(j):
            copy.start()
        kbuf[0, j] = normed_keys(total[:, :HD])
        vbuf[0, j] = total[:, HD : 2 * HD].astype(jnp.bfloat16)

    def project_step(c):
        for copy in weight_copies(c):
            copy.wait()
        patch_copy(c).wait()
        project_pair(c)

    def project_image(j):
        patch_copy(CHUNKS + j - 2).wait()
        keep_kv(j, jnp.dot(xbuf[j], wbuf[...], preferred_element_type=jnp.float32))

    project_step(0)
    pl.semaphore_wait(barrier, XS - 1 + len(z_mates))
    for n in (2, 1, 0):
        for copy in query_z(n):
            copy.start()
    forward(0)
    for c in range(1, CHUNKS):
        project_step(c)
    for j in range(2):
        keep_kv(j, raw[j * rows : (j + 1) * rows, :])
    project_image(2)
    project_image(3)
    forward(1)
    forward(3)
    forward(2)
    for j in range(images):
        for copy in kv_copies(j):
            copy.wait_recv()

    row = lax.broadcasted_iota(jnp.int32, (HD, HD), 0)
    column_of = lax.broadcasted_iota(jnp.int32, (HD, HD), 1)
    diagonal = row == column_of
    lane_value = column_of.astype(jnp.float32)

    def attend(dz):
        pair = lax.rem(zh + dz, pairs)
        chosen = []
        for column in range(XS):
            spread = jnp.broadcast_to(ids[pair, column], (ROWS, HD))
            image = jnp.sum(
                jnp.where(diagonal[:ROWS], spread, 0.0), axis=1, keepdims=True
            )
            chosen.append(jnp.where(lane_value[:ROWS] == image, 1.0, 0.0).astype(jnp.bfloat16))
        asked = jnp.concatenate(
            [qx[pair].reshape(XS * ROWS, HD), jnp.concatenate(chosen, axis=0)], axis=1
        )
        weights, worth = [], []
        for half in range(CORES):
            for j in range(images):
                scores = lax.dot_general(
                    asked,
                    jnp.concatenate([kbuf[half, j], kext[half, j]], axis=1),
                    (((1,), (1,)), ((), ())),
                    preferred_element_type=jnp.float32,
                )
                weights.append(jnp.exp2(scores).astype(jnp.bfloat16))
                value = vbuf[half, j]
                worth.append(jnp.concatenate([value, jnp.ones_like(value)], axis=1))
        total = jnp.dot(
            jnp.concatenate(weights, axis=1),
            jnp.concatenate(worth, axis=0),
            preferred_element_type=jnp.float32,
        )
        mnum[dz] = total[:, :HD].astype(jnp.bfloat16).reshape(XS, ROWS, HD)
        for part in range(2):
            below = total[part * HD : (part + 1) * HD, HD:]
            mden[dz, part] = jnp.sum(
                jnp.where(diagonal, below, 0.0), axis=0, keepdims=True
            )
        for o in (2, 1, 3):
            for copy in result_x(o, dz):
                copy.start()

    def result_x(o, dz):
        column = lax.rem(x + o, XS)
        return [
            pltpu.make_async_remote_copy(
                src_ref=source,
                dst_ref=into.at[dz, o],
                send_sem=rx_send.at[dz, o, i],
                recv_sem=rx_recv.at[dz, o, i],
                device_id=x_mate(o),
                device_id_type=MESH,
            )
            for i, (source, into) in enumerate(
                ((mnum.at[dz, column], xnum), (mden.at[dz, column // 2], xden))
            )
        ]

    def query_x_wait(dz):
        for o in (1, 3, 2):
            for copy in query_x(o, dz, back=True):
                copy.wait_recv()

    flips = [(zf, cf) for zf in range(2) for cf in range(CORES)]

    def result_z(dz, zf, cf):
        pair = lax.rem(zh + dz, pairs)
        chip = lax.rem(zl + zf, 2)
        side = lax.rem(core + cf, CORES)
        part = chip * CORES + side
        return [
            pltpu.make_async_remote_copy(
                src_ref=source,
                dst_ref=into.at[core, dz, zf],
                send_sem=rz_send.at[dz, zf, cf, i],
                recv_sem=rz_recv.at[dz, zf, cf, i],
                device_id={"wide": pair * XS + x, "depth": part},
                device_id_type=MESH,
            )
            for i, (source, into) in enumerate(
                ((znum.at[dz, part], gnum), (zden.at[dz], gden))
            )
        ]

    def pass_on(dz):
        number = mnum[dz, x].astype(jnp.float32)
        below = mden[dz, x // 2]
        for o in (1, 3, 2):
            for copy in result_x(o, dz):
                copy.wait_recv()
            number = number + xnum[dz, o].astype(jnp.float32)
            below = below + xden[dz, o]
        znum[dz] = number.astype(jnp.bfloat16).reshape(2 * CORES, 16, HD)
        zden[dz] = below
        for zf, cf in flips:
            if dz or zf or cf:
                for copy in result_z(dz, zf, cf):
                    copy.start()

    query_x_wait(0)
    attend(0)
    query_x_wait(1)
    attend(1)
    query_x_wait(3)
    attend(3)
    query_x_wait(2)
    attend(2)
    pass_on(0)
    pass_on(1)
    pass_on(3)
    pass_on(2)
    gnum[core, 0, 0] = znum[0, depth]
    gden[core, 0, 0] = zden[0]
    for dz in (0, 1, 3, 2):
        for zf, cf in flips:
            if dz or zf or cf:
                for copy in result_z(dz, zf, cf):
                    copy.wait_recv()
    place = lax.rem(x, 2) * ROWS + depth * 16
    here = column_of[:16] == row[:16] + place
    for k in range(CORES):
        number = jnp.zeros((16, HD), jnp.float32)
        below = jnp.zeros((1, HD), jnp.float32)
        for dz in range(pairs):
            for zf in range(2):
                number = number + gnum[k, dz, zf].astype(jnp.float32)
                below = below + gden[k, dz, zf]
        spread = jnp.where(here, jnp.broadcast_to(below, (16, HD)), 0.0)
        res[...] = number / jnp.sum(spread, axis=1, keepdims=True)
        for h in range(GROUP):
            out[:, pl.ds((k * GROUP + h) * HD, HD)] = res[pl.ds(h * SHARE, SHARE), :].astype(
                out.dtype
            )
    for n in range(3):
        for copy in query_z(n):
            copy.wait_send()
    for dz in range(pairs):
        for o in range(1, XS):
            for copy in query_x(o, dz) + result_x(o, dz):
                copy.wait_send()
        for zf, cf in flips:
            if dz or zf or cf:
                for copy in result_z(dz, zf, cf):
                    copy.wait_send()
    for j in range(images):
        for copy in kv_copies(j):
            copy.wait_send()


def local(
    patch_store,
    w_key,
    w_value,
    key_gain,
    query_gain,
    queries,
    owner_table,
    reader_table,
    request_image,
    image_tiles,
):
    images, rows, width = patch_store.shape
    batch, q_cols = queries.shape
    anywhere = pl.BlockSpec(memory_space=pl.ANY)
    dma = pltpu.SemaphoreType.DMA
    bf16, f32 = jnp.bfloat16, jnp.float32
    pairs = ZS // 2
    return pl.pallas_call(
        kernel,
        out_shape=pltpu.VMEM((SHARE, q_cols), bf16),
        in_specs=[anywhere] * 10,
        out_specs=pl.BlockSpec(memory_space=pltpu.VMEM),
        scratch_shapes=[
            pltpu.SMEM(owner_table.shape, jnp.int32),
            pltpu.SMEM(reader_table.shape[::-1], jnp.int32),
            pltpu.SMEM(request_image.shape, jnp.int32),
            pltpu.SMEM(image_tiles.shape, jnp.int32),
            pltpu.VMEM((images, rows, width), bf16),
            pltpu.VMEM((width, 4 * HD), bf16),
            pltpu.VMEM((batch, GROUP * HD), bf16),
            pltpu.VMEM((2, 1, HD), f32),
            pltpu.VMEM((GROUP, batch, HD), f32),
            pltpu.VMEM((ROWS, HD), f32),
            pltpu.VMEM((pairs, XS, ROWS, HD), bf16),
            pltpu.VMEM((pairs, XS, 1, HD), f32),
            pltpu.VMEM((2 * rows, 4 * HD), f32),
            pltpu.VMEM((2, images, rows, HD), bf16),
            pltpu.VMEM((CORES, images, rows, HD), bf16),
            pltpu.VMEM((CORES, images, rows, HD), bf16),
            pltpu.VMEM((CORES, images, rows, HD), bf16),
            pltpu.VMEM((pairs, XS, ROWS, HD), bf16),
            pltpu.VMEM((pairs, 2, 1, HD), f32),
            pltpu.VMEM((pairs, XS, ROWS, HD), bf16),
            pltpu.VMEM((pairs, XS, 1, HD), f32),
            pltpu.VMEM((pairs, 2 * CORES, 16, HD), bf16),
            pltpu.VMEM((pairs, 1, HD), f32),
            pltpu.VMEM((CORES, pairs, 2, 16, HD), bf16),
            pltpu.VMEM((CORES, pairs, 2, 1, HD), f32),
            pltpu.VMEM((16, HD), f32),
            dma((2, CHUNKS, 2)),
            dma((CHUNKS + images - 2,)),
            dma((7,)),
            dma((3, 2)),
            dma((pairs, 2)),
            dma((XS, pairs, 2)),
            dma((XS, pairs, 2)),
            dma((2, images)),
            dma((2, images)),
            dma((pairs, XS, 2)),
            dma((pairs, XS, 2)),
            dma((pairs, 2, CORES, 2)),
            dma((pairs, 2, CORES, 2)),
        ],
        compiler_params=pltpu.CompilerParams(
            collective_id=0, has_side_effects=True, vmem_limit_bytes=56 * 1024 * 1024
        ),
    )(
        patch_store,
        w_key,
        w_value,
        key_gain.reshape(1, HD),
        query_gain.reshape(1, HD),
        queries,
        owner_table,
        reader_table.T,
        request_image,
        image_tiles,
    )


def solution(mesh):
    placed = (
        P("wide", "depth", None),
        P(None, "narrow"),
        P(None, "narrow"),
        P(),
        P(),
        P("wide", "narrow"),
        P(),
        P(),
        P("wide"),
        P(),
    )
    return jax.shard_map(
        local,
        mesh=mesh,
        in_specs=placed,
        out_specs=P(("wide", "depth"), "narrow"),
        check_vma=False,
    )
```

time: 37.1 us -> 31.8 us (0.86)
  Pallas kernels: 35 us -> 31.1 us
  local copies, waits for them, and re-layouts: 1.95 us -> 0.6 us
    pallas_call x1, Pallas kernels: 35 us -> 31.1 us  [local(): pl.pallas_call(kernel, out_shape=pltpu.VMEM((SHARE, q_cols), bf16), in_sp...]
    unnamed x2 -> x1, local copies, waits for them, and re-layouts: 1.95 us -> 0.6 us
where the time goes in v2:
time: 31.8 us
  Pallas kernels  31.1 us (98%)
  local copies, waits for them, and re-layouts  0.6 us (2%)
    pallas_call x1, Pallas kernels, local(): pl.pallas_call(kernel, out_shape=pltpu.VMEM((SHARE, q_cols), bf16), in_sp...  31.1 us

profile of v2, /device:TPU:1, one launch (start us, length us, event | category | flops | bytes accessed | tf_op | source)
XLA Modules:
  0.0 31.8 jit_solution(17172400360967046135)
XLA Ops:
  0.0 31.1 %shard_map.100 = bf16[4,1024]{1,0:T(4,128)(2,1)S(1)} custom-call(bf16[4,256,4096]{2,1,0:T(8,128)(2,1)} %store.1, bf16[4096,256]{1,0:T(8,128)(2,1)} %w_key.1, bf16[4096,256]{1,0:T(8,128)(2,1)} %w_value.1, f32[1,128]{1,0:T(1,128)} %bitcast.4, f32[1,128]{1,0:T(1,128)} %bitcast.5, bf16[16,1024]{1,0:T(8,128)(2,1)} %queries.1, s32[64]{0:T(128)} %owner_hbm.1, ...), custom_call_target="tpu_custom_call" | custom-call | tf_op jit(solution)/shard_map/pallas_call | solution.py:464
  31.2 0.6 %copy.12 = bf16[4,1024]{1,0:T(4,128)(2,1)} copy(bf16[4,1024]{1,0:T(4,128)(2,1)S(1)} %shard_map.100) | data formatting | bytes 16384

commit v3 on v2

--- a/solution.py
+++ b/solution.py
@@ -58,6 +58,7 @@
     zden,
     gnum,
     gden,
+    wide_raw,
     res,
     w_sem,
     x_sem,
@@ -72,6 +73,7 @@
     rx_recv,
     rz_send,
     rz_recv,
+    near_sem,
 ):
     images, rows, width = xbuf.shape
     batch = qraw.shape[0]
@@ -93,12 +95,17 @@
         part = lax.rem(there, 2) * CORES + lax.rem(core + dc, CORES)
         return {"wide": there // 2 * XS + x, "depth": part}
 
-    z_mates = [(dz, dc) for dz in range(ZS) for dc in range(CORES) if dz or dc]
-
-    for o in range(1, XS):
-        pl.semaphore_signal(barrier, inc=1, device_id=x_mate(o), device_id_type=MESH)
-    for dz, dc in z_mates:
-        pl.semaphore_signal(barrier, inc=1, device_id=z_mate(dz, dc), device_id_type=MESH)
+    toward = jnp.where(zl == 1, 1, ZS - 1)
+    greeted = [x_mate(o) for o in range(1, XS)] + [
+        z_mate(0, 1),
+        z_mate(toward, 0),
+        z_mate(2 * toward, 0),
+        z_mate(3 * toward, 0),
+        z_mate(ZS * 2 - 2 * toward, 0),
+    ]
+
+    for device in greeted:
+        pl.semaphore_signal(barrier, inc=1, device_id=device, device_id_type=MESH)
 
     def head_lanes(which):
         return pl.ds(pl.multiple_of(which * HD, HD), HD)
@@ -132,17 +139,16 @@
         pltpu.make_async_copy(request_hbm, request_image, small_sem.at[5]),
         pltpu.make_async_copy(tiles_hbm, image_tiles, small_sem.at[6]),
     ]
-    for copy in small:
-        copy.start()
-    for c in range(CHUNKS):
+    def start_piece(c):
         for copy in weight_copies(c):
             copy.start()
         patch_copy(c).start()
-    for j in range(2, images):
-        patch_copy(CHUNKS + j - 2).start()
+
     for copy in small:
+        copy.start()
+    start_piece(0)
+    for copy in small[:3]:
         copy.wait()
-
     gain = gains[0] * gains[1] * (math.log2(math.e) / math.sqrt(HD))
     for h in range(GROUP):
         head = qraw[:, h * HD : (h + 1) * HD].astype(jnp.float32)
@@ -153,6 +159,12 @@
             qs[pl.ds(t * 16 + h * SHARE, SHARE), :] = qf[h, pl.ds(t * SHARE, SHARE), :]
     qx[zh, x] = qs[...].astype(jnp.bfloat16)
 
+    for c in range(1, CHUNKS):
+        start_piece(c)
+    for j in range(2, images):
+        patch_copy(CHUNKS + j - 2).start()
+    for copy in small[3:]:
+        copy.wait()
     lane = lax.broadcasted_iota(jnp.int32, (1, HD), 1)
     request = lax.rem(lane, ROWS) // 16 * SHARE + lax.rem(lane, SHARE)
     first, second = reader_table[0, wide], reader_table[1, wide]
@@ -269,12 +281,13 @@
         patch_copy(c).wait()
         project_pair(c)
 
-    def project_image(j):
-        patch_copy(CHUNKS + j - 2).wait()
-        keep_kv(j, jnp.dot(xbuf[j], wbuf[...], preferred_element_type=jnp.float32))
+    def project_rows(j, start, count):
+        return jnp.dot(
+            xbuf[j, start : start + count, :], wbuf[...], preferred_element_type=jnp.float32
+        )
 
     project_step(0)
-    pl.semaphore_wait(barrier, XS - 1 + len(z_mates))
+    pl.semaphore_wait(barrier, len(greeted))
     for n in (2, 1, 0):
         for copy in query_z(n):
             copy.start()
@@ -283,21 +296,23 @@
         project_step(c)
     for j in range(2):
         keep_kv(j, raw[j * rows : (j + 1) * rows, :])
-    project_image(2)
-    project_image(3)
+    patch_copy(CHUNKS).wait()
+    keep_kv(2, project_rows(2, 0, rows))
     forward(1)
     forward(3)
+    patch_copy(CHUNKS + 1).wait()
+    raw[:128, :] = project_rows(3, 0, 128)
     forward(2)
-    for j in range(images):
-        for copy in kv_copies(j):
-            copy.wait_recv()
+    pl.semaphore_signal(near_sem, inc=1, device_id=z_mate(0, 1), device_id_type=MESH)
+    raw[128:256, :] = project_rows(3, 128, 128)
+    keep_kv(3, raw[:256, :])
 
     row = lax.broadcasted_iota(jnp.int32, (HD, HD), 0)
     column_of = lax.broadcasted_iota(jnp.int32, (HD, HD), 1)
     diagonal = row == column_of
     lane_value = column_of.astype(jnp.float32)
 
-    def attend(dz):
+    def asked_of(dz):
         pair = lax.rem(zh + dz, pairs)
         chosen = []
         for column in range(XS):
@@ -306,11 +321,13 @@
                 jnp.where(diagonal[:ROWS], spread, 0.0), axis=1, keepdims=True
             )
             chosen.append(jnp.where(lane_value[:ROWS] == image, 1.0, 0.0).astype(jnp.bfloat16))
-        asked = jnp.concatenate(
+        return jnp.concatenate(
             [qx[pair].reshape(XS * ROWS, HD), jnp.concatenate(chosen, axis=0)], axis=1
         )
+
+    def weigh(asked, halves):
         weights, worth = [], []
-        for half in range(CORES):
+        for half in halves:
             for j in range(images):
                 scores = lax.dot_general(
                     asked,
@@ -321,11 +338,13 @@
                 weights.append(jnp.exp2(scores).astype(jnp.bfloat16))
                 value = vbuf[half, j]
                 worth.append(jnp.concatenate([value, jnp.ones_like(value)], axis=1))
-        total = jnp.dot(
+        return jnp.dot(
             jnp.concatenate(weights, axis=1),
             jnp.concatenate(worth, axis=0),
             preferred_element_type=jnp.float32,
         )
+
+    def send_x(dz, total):
         mnum[dz] = total[:, :HD].astype(jnp.bfloat16).reshape(XS, ROWS, HD)
         for part in range(2):
             below = total[part * HD : (part + 1) * HD, HD:]
@@ -335,6 +354,9 @@
         for o in (2, 1, 3):
             for copy in result_x(o, dz):
                 copy.start()
+
+    def attend(dz):
+        send_x(dz, weigh(asked_of(dz), range(CORES)))
 
     def result_x(o, dz):
         column = lax.rem(x + o, XS)
@@ -394,17 +416,22 @@
                     copy.start()
 
     query_x_wait(0)
-    attend(0)
-    query_x_wait(1)
-    attend(1)
-    query_x_wait(3)
-    attend(3)
+    wide_raw[...] = weigh(asked_of(0), (0,))
+    for j in range(images):
+        for copy in kv_copies(j):
+            copy.wait_recv()
+    send_x(0, wide_raw[...] + weigh(asked_of(0), (1,)))
     query_x_wait(2)
     attend(2)
+    query_x_wait(1)
+    query_x_wait(3)
+    attend(1)
+    pl.semaphore_wait(near_sem, 1)
     pass_on(0)
+    attend(3)
+    pass_on(2)
     pass_on(1)
     pass_on(3)
-    pass_on(2)
     gnum[core, 0, 0] = znum[0, depth]
     gden[core, 0, 0] = zden[0]
     for dz in (0, 1, 3, 2):
@@ -492,6 +519,7 @@
             pltpu.VMEM((pairs, 1, HD), f32),
             pltpu.VMEM((CORES, pairs, 2, 16, HD), bf16),
             pltpu.VMEM((CORES, pairs, 2, 1, HD), f32),
+            pltpu.VMEM((XS * ROWS, 2 * HD), f32),
             pltpu.VMEM((16, HD), f32),
             dma((2, CHUNKS, 2)),
             dma((CHUNKS + images - 2,)),
@@ -506,6 +534,7 @@
             dma((pairs, XS, 2)),
             dma((pairs, 2, CORES, 2)),
             dma((pairs, 2, CORES, 2)),
+            pltpu.SemaphoreType.REGULAR,
         ],
         compiler_params=pltpu.CompilerParams(
             collective_id=0, has_side_effects=True, vmem_limit_bytes=56 * 1024 * 1024

time: 31.8 us -> 30.4 us (0.956)
  Pallas kernels: 31.1 us -> 29.7 us
    pallas_call x1, Pallas kernels: 31.1 us -> 29.7 us  [local(): pl.pallas_call(kernel, out_shape=pltpu.VMEM((SHARE, q_cols), bf16), in_sp...]
where the time goes in v3:
time: 30.4 us; the launch traced here: 30.3 us
  Pallas kernels  29.7 us (98%)
  local copies, waits for them, and re-layouts  0.6 us (2%)
    pallas_call x1, Pallas kernels, local(): pl.pallas_call(kernel, out_shape=pltpu.VMEM((SHARE, q_cols), bf16), in_sp...  29.7 us

profile of v3, /device:TPU:1, one launch (start us, length us, event | category | flops | bytes accessed | tf_op | source)
XLA Modules:
  0.0 30.3 jit_solution(482767960294614306)
XLA Ops:
  0.0 29.7 %shard_map.100 = bf16[4,1024]{1,0:T(4,128)(2,1)S(1)} custom-call(bf16[4,256,4096]{2,1,0:T(8,128)(2,1)} %store.1, bf16[4096,256]{1,0:T(8,128)(2,1)} %w_key.1, bf16[4096,256]{1,0:T(8,128)(2,1)} %w_value.1, f32[1,128]{1,0:T(1,128)} %bitcast.4, f32[1,128]{1,0:T(1,128)} %bitcast.5, bf16[16,1024]{1,0:T(8,128)(2,1)} %queries.1, s32[64]{0:T(128)} %owner_hbm.1, ...), custom_call_target="tpu_custom_call" | custom-call | tf_op jit(solution)/shard_map/pallas_call | solution.py:491
  29.7 0.6 %copy.12 = bf16[4,1024]{1,0:T(4,128)(2,1)} copy(bf16[4,1024]{1,0:T(4,128)(2,1)S(1)} %shard_map.100) | data formatting | bytes 16384
